TPU v7x, 32 devices: a whole 2x2x4 slice. The times are simulated.
32 devices in a mesh: tm: 8 (over z, y), space: 4 (over x, core).
Axes of the slice: x: 2, y: 2, z: 4, core: 2. Of those that a mesh axis runs over, the one named last changes fastest.
Arguments:
- states: float32 [8, 3, 256, 1024], P('tm', None, 'space'), may hold values from -3 to 3
- background: float32 [3, 256, 1024], P(None, 'space'), may hold values from -3 to 3
- obs_cells: int32 [8, 4, 1024], P('tm'), may hold values from 0 to 262143
- obs_values: float32 [8, 4, 1024], P('tm'), may hold values from -3 to 3
- land_mask: int32 [256, 1024], P('space'), may hold values 0 or 1
Outputs:
- gradient: float32 [8, 3, 256, 1024], P('tm', None, 'space')
- next_states: float32 [8, 3, 256, 1024], P('tm', None, 'space')
All inputs are finite; a program needn't handle non-finite values. No bound on the sum of `land_mask` on one device may be relied on, other than what follows from the above.
Results may differ from a plain program's by a relative error of at most 0.0003.
Values sent between devices are 32-bit elements; how exact they have to be, the bound alone decides.
A program may use at most 64 MiB of HBM per device.

v0:
```python
import functools

import jax
import jax.numpy as jnp
from jax import lax
from jax.experimental import pallas as pl
from jax.experimental.pallas import tpu as pltpu
from jax.sharding import PartitionSpec as P

NSTEP = 4
PAD = 8

advect = 0.25
gravity = 1.0
coriolis = 0.1
diffuse = 0.1
defect_weight = 2.0
obs_weight = 4.0
step_length = 0.1

KEEP = 1.0 - 4.0 * diffuse
HALF = advect / 2.0
HALF_G = advect * gravity / 2.0

MESH = pl.DeviceIdType.MESH


def kernel(
    n_tm,
    n_sp,
    states,
    background,
    cells,
    values,
    land,
    gradient,
    nexts,
    xt,
    yt,
    z0,
    prev_end,
    lam_a,
    lam_b,
    land_i,
    mask,
    dense_x,
    dense_y,
    cells_n,
    values_n,
    send,
    recv,
):
    rows, cols = states.shape[1], states.shape[2]
    tm, sp = lax.axis_index("tm"), lax.axis_index("space")
    wide = rows + 2 * PAD
    tiles = wide // PAD
    low, high = 2 * PAD, 2 * PAD + rows
    has_next, has_next2 = tm < n_tm - 1, tm < n_tm - 2
    has_prev, has_prev2 = tm > 0, tm > 1
    has_up, has_down = sp > 0, sp < n_sp - 1

    def span(t):
        return pl.ds(pl.multiple_of(t * PAD, PAD), PAD)

    for start in (0, PAD, high, high + PAD):
        blank = jnp.zeros((3, PAD, cols), jnp.float32)
        for ref in (xt.at[0], yt.at[0], z0):
            ref[:, start : start + PAD] = blank
        land_i[start : start + PAD] = jnp.zeros((PAD, cols), jnp.int32)

    barrier = pltpu.get_barrier_semaphore()
    near = (
        (has_up, (tm, sp - 1)),
        (has_down, (tm, sp + 1)),
        (has_prev, (tm - 1, sp)),
        (has_next, (tm + 1, sp)),
        (has_prev2, (tm - 2, sp)),
        (has_next2, (tm + 2, sp)),
    )
    for there, device in near:

        @pl.when(there)
        def _(device=device):
            pl.semaphore_signal(barrier, inc=1, device_id=device, device_id_type=MESH)

    pl.semaphore_wait(barrier, sum(there.astype(jnp.int32) for there, _ in near))

    def copy(index, src, dst, device):
        return pltpu.make_async_remote_copy(
            src_ref=src,
            dst_ref=dst,
            send_sem=send.at[index],
            recv_sem=recv.at[index],
            device_id=device,
            device_id_type=MESH,
        )

    started = []

    def start(index, src, dst, device, sends, receives):
        entry = copy(index, src, dst, device)

        @pl.when(sends)
        def _():
            entry.start()

        started.append((entry, sends))
        return entry, receives

    def arrive(*pairs):
        for entry, receives in pairs:

            @pl.when(receives)
            def _(entry=entry):
                entry.wait_recv()

    above, below = (tm, sp - 1), (tm, sp + 1)
    back, back2, ahead = (tm - 1, sp), (tm - 2, sp), (tm + 1, sp)
    yes_up, yes_down = has_up, has_down
    head, tail = pl.ds(0, PAD), pl.ds(rows - PAD, PAD)
    x0, y0 = xt.at[0], yt.at[0]
    top, bottom = pl.ds(PAD, PAD), pl.ds(high, PAD)
    y_head, y_tail = pl.ds(low, PAD), pl.ds(high - PAD, PAD)

    halo = [
        start(0, states.at[:, head], x0.at[:, bottom], above, yes_up, yes_down),
        start(1, states.at[:, tail], x0.at[:, top], below, yes_down, yes_up),
        start(2, land.at[head], land_i.at[bottom], above, yes_up, yes_down),
        start(3, land.at[tail], land_i.at[top], below, yes_down, yes_up),
    ]
    even = lax.rem(tm, 2) == 0
    odd = jnp.logical_not(even)
    obs_next = [
        start(4, cells, cells_n, back, has_prev, has_next),
        start(5, values, values_n, back, has_prev, has_next),
    ]
    pieces = [0, rows - PAD, *range(PAD, rows - PAD, PAD)]
    n_piece = len(pieces)
    source = [pl.ds(row, PAD) for row in pieces]
    target = [pl.ds(low + row, PAD) for row in pieces]
    far = [
        start(8 + i, states.at[:, source[i]], z0.at[:, target[i]], back2, has_prev2, has_next2)
        for i in range(n_piece)
    ]
    direct = [
        start(
            8 + n_piece + i,
            states.at[:, source[i]],
            y0.at[:, target[i]],
            back,
            odd,
            even & has_next,
        )
        for i in range(n_piece)
    ]
    relayed = []

    def relay(count):
        for i in range(len(relayed), min(len(relayed) + count, n_piece)):
            arrive(far[i])
            relayed.append(
                start(
                    8 + 2 * n_piece + i,
                    z0.at[:, target[i]],
                    y0.at[:, target[i]],
                    ahead,
                    even & has_next2,
                    odd & has_next,
                )
            )

    first_row = sp * rows - PAD
    shift = cols.bit_length() - 1

    def densify(cells, values, dense, begin_at, end_at):
        width = min(cols, 256)

        def one(s, carry):
            cell = cells[pl.ds(s, 1), :]
            value = values[pl.ds(s, 1), :]
            row = lax.shift_right_logical(cell, shift) - first_row
            col = lax.bitwise_and(cell, cols - 1)
            count = cell.shape[1]
            level = lax.broadcasted_iota(jnp.int32, (wide, count), 0)
            hit = level == row
            upper = value.astype(jnp.bfloat16).astype(jnp.float32)
            lower = value - upper
            picks = jnp.concatenate(
                [
                    jnp.where(hit, 1.0, 0.0),
                    jnp.where(hit, upper, 0.0),
                    jnp.where(hit, lower, 0.0),
                ],
                axis=0,
            ).astype(jnp.bfloat16)

            def part(c, carry):
                place = pl.multiple_of(c * width, width)
                column = lax.broadcasted_iota(jnp.int32, (width, count), 0) + place
                spread = jnp.where(column == col, 1.0, 0.0).astype(jnp.bfloat16)
                out = lax.dot_general(
                    picks, spread, (((1,), (1,)), ((), ())), preferred_element_type=jnp.float32
                )
                dense[s, 0, PAD : PAD + wide, pl.ds(place, width)] = obs_weight * out[:wide]
                dense[s, 1, PAD : PAD + wide, pl.ds(place, width)] = obs_weight * (
                    out[wide : 2 * wide] + out[2 * wide :]
                )
                return carry

            return lax.fori_loop(0, cols // width, part, carry)

        lax.fori_loop(begin_at, end_at, one, 0)

    sub = lax.broadcasted_iota(jnp.int32, (PAD, cols), 0)
    is_first, is_last = sub == 0, sub == PAD - 1

    def valid(t):
        row = sub + (first_row + (t - 1) * PAD)
        return jnp.where((row >= 0) & (row < rows * n_sp), 1.0, 0.0)

    def around(ref, field, t):
        here = ref[field, span(t), :]
        before = ref[field, span(t - 1), :]
        after = ref[field, span(t + 1), :]
        up = pltpu.roll(jnp.where(is_last, before, here), 1, 0)
        down = pltpu.roll(jnp.where(is_first, after, here), PAD - 1, 0)
        left = pltpu.roll(here, 1, 1)
        right = pltpu.roll(here, cols - 1, 1)
        return here, up, down, left, right

    def forward(levels):
        def step(s, carry):
            src, dst = levels.at[s], levels.at[s + 1]

            def tile(t, carry):
                h, hu, hd, hl, hr = around(src, 0, t)
                u, uu, ud, ul, ur = around(src, 1, t)
                v, vu, vd, vl, vr = around(src, 2, t)
                m = mask[span(t), :]
                flux = (1.0 + hr) * ur - (1.0 + hl) * ul + (1.0 + hd) * vd - (1.0 + hu) * vu
                dst[0, span(t), :] = valid(t) * (
                    KEEP * h - HALF * flux + diffuse * ((hu + hd) + (hl + hr))
                )
                dst[1, span(t), :] = m * (
                    KEEP * u
                    - HALF_G * (hr - hl)
                    + coriolis * v
                    + diffuse * ((uu + ud) + (ul + ur))
                )
                dst[2, span(t), :] = m * (
                    KEEP * v
                    - HALF_G * (hd - hu)
                    - coriolis * u
                    + diffuse * ((vu + vd) + (vl + vr))
                )
                return carry

            return lax.fori_loop(1, tiles + 1, tile, carry)

        lax.fori_loop(0, NSTEP, step, 0)

    def begin(levels, following, there, dense, lam):
        def tile(t, carry):
            m = mask[span(t), :]
            ends = levels.at[NSTEP]

            def drive(field):
                defect = following[field, span(t), :] - ends[field, span(t), :]
                return jnp.where(there, -defect_weight * defect, 0.0)

            push = dense[NSTEP - 1, 0, span(t), :] * ends[0, span(t), :]
            push = push - dense[NSTEP - 1, 1, span(t), :]
            lam[0, span(t), :] = valid(t) * (drive(0) + push)
            lam[1, span(t), :] = m * drive(1)
            lam[2, span(t), :] = m * drive(2)
            return carry

        lax.fori_loop(1, tiles + 1, tile, 0)

    def adjoint_tile(src, state, t):
        p, pu, pd, pleft, pr = around(src, 0, t)
        q, qu, qd, ql, qr = around(src, 1, t)
        r, ru, rd, rl, rr = around(src, 2, t)
        depth = 1.0 + state[0, span(t), :]
        dx = HALF * (pr - pleft)
        dy = HALF * (pd - pu)
        lam_h = (
            KEEP * p
            + diffuse * ((pu + pd) + (pleft + pr))
            + state[1, span(t), :] * dx
            + state[2, span(t), :] * dy
            + HALF_G * ((qr - ql) + (rd - ru))
        )
        lam_u = KEEP * q + diffuse * ((qu + qd) + (ql + qr)) + depth * dx - coriolis * r
        lam_v = KEEP * r + diffuse * ((ru + rd) + (rl + rr)) + depth * dy + coriolis * q
        return lam_h, lam_u, lam_v

    def adjoint(levels, dense):
        src, dst = lam_a, lam_b
        for s in reversed(range(1, NSTEP)):

            def tile(t, carry, src=src, dst=dst, s=s):
                lam_h, lam_u, lam_v = adjoint_tile(src, levels.at[s], t)
                push = dense[s - 1, 0, span(t), :] * levels[s, 0, span(t), :]
                push = push - dense[s - 1, 1, span(t), :]
                m = mask[span(t), :]
                dst[0, span(t), :] = valid(t) * (lam_h + push)
                dst[1, span(t), :] = m * lam_u
                dst[2, span(t), :] = m * lam_v
                return carry

            lax.fori_loop(1, tiles + 1, tile, 0)
            src, dst = dst, src
        return src

    def place(t, carry):
        x0[:, span(t + 2), :] = states[:, span(t), :]
        land_i[span(t + 2), :] = land[span(t), :]
        return carry

    lax.fori_loop(0, rows // PAD, place, 0)
    half = NSTEP // 2
    densify(cells, values, dense_x, 0, NSTEP)
    arrive(*halo)

    def to_mask(t, carry):
        mask[span(t), :] = land_i[span(t), :].astype(jnp.float32)
        return carry

    lax.fori_loop(0, tiles + 2, to_mask, 0)
    relay(2)
    forward(xt)
    relay(2)
    arrive(*obs_next)
    densify(cells_n, values_n, dense_y, 0, half)
    relay(1)
    densify(cells_n, values_n, dense_y, half, NSTEP)
    relay(1)
    arrive(*direct[:2], *relayed[:2])
    next_up = has_next & has_up
    next_down = has_next & has_down
    next2_up = has_next2 & has_up
    next2_down = has_next2 & has_down
    halo_next = [
        start(6, y0.at[:, y_head], y0.at[:, bottom], above, next_up, next_down),
        start(7, y0.at[:, y_tail], y0.at[:, top], below, next_down, next_up),
    ]
    base = 8 + 3 * n_piece
    halo_far = [
        start(base, z0.at[:, y_head], z0.at[:, bottom], above, next2_up, next2_down),
        start(base + 1, z0.at[:, y_tail], z0.at[:, top], below, next2_down, next2_up),
    ]
    relay(n_piece)
    ends = start(
        base + 2, xt.at[NSTEP, :, pl.ds(low, rows)], prev_end, ahead, has_next, has_prev
    )
    arrive(*direct[2:], *relayed[2:], *halo_next)

    begin(xt, y0, has_next, dense_x, lam_a)
    last = adjoint(xt, dense_x)

    def own(t, carry):
        lam = adjoint_tile(last, x0, t)
        for field in range(3):
            gradient[field, span(t - 2), :] = lam[field]
        return carry

    lax.fori_loop(2, tiles, own, 0)

    forward(yt)
    arrive(*halo_far)
    begin(yt, z0, has_next2, dense_y, lam_a)
    last = adjoint(yt, dense_y)

    def other(t, carry):
        lam = adjoint_tile(last, y0, t)
        for field in range(3):
            state = y0[field, span(t), :]
            end = xt[NSTEP, field, span(t), :]
            grad = defect_weight * (state - end) + lam[field]
            nexts[field, span(t - 2), :] = jnp.where(has_next, state - step_length * grad, end)
        return carry

    lax.fori_loop(2, tiles, other, 0)

    arrive(ends)

    def finish(t, carry):
        for field in range(3):
            before = jnp.where(
                has_prev, prev_end[field, span(t), :], background[field, span(t), :]
            )
            defect = states[field, span(t), :] - before
            gradient[field, span(t), :] = gradient[field, span(t), :] + defect_weight * defect
        return carry

    lax.fori_loop(0, rows // PAD, finish, 0)

    for entry, sends in started:

        @pl.when(sends)
        def _(entry=entry):
            entry.wait_send()


def solution(mesh):
    n_tm, n_sp = mesh.shape["tm"], mesh.shape["space"]

    def local(states, background, obs_cells, obs_values, land_mask):
        _, fields, rows, cols = states.shape
        padded = rows + 4 * PAD
        block = jax.ShapeDtypeStruct((fields, rows, cols), jnp.float32)
        f32 = functools.partial(pltpu.VMEM, dtype=jnp.float32)
        gradient, nexts = pl.pallas_call(
            functools.partial(kernel, n_tm, n_sp),
            out_shape=(block, block),
            in_specs=[pl.BlockSpec(memory_space=pltpu.VMEM)] * 5,
            out_specs=(pl.BlockSpec(memory_space=pltpu.VMEM),) * 2,
            scratch_shapes=[
                f32((NSTEP + 1, fields, padded, cols)),
                f32((NSTEP + 1, fields, padded, cols)),
                f32((fields, padded, cols)),
                f32((fields, rows, cols)),
                f32((fields, padded, cols)),
                f32((fields, padded, cols)),
                pltpu.VMEM((padded, cols), jnp.int32),
                f32((padded, cols)),
                f32((NSTEP, 2, padded, cols)),
                f32((NSTEP, 2, padded, cols)),
                pltpu.VMEM(obs_cells.shape[1:], jnp.int32),
                f32(obs_values.shape[1:]),
                pltpu.SemaphoreType.DMA((11 + 3 * (rows // PAD),)),
                pltpu.SemaphoreType.DMA((11 + 3 * (rows // PAD),)),
            ],
            compiler_params=pltpu.CompilerParams(
                collective_id=0, has_side_effects=True, vmem_limit_bytes=60 * 2**20
            ),
        )(states[0], background, obs_cells[0], obs_values[0], land_mask)
        return gradient[None], nexts[None]

    in_specs = (
        P("tm", None, "space", None),
        P(None, "space", None),
        P("tm", None, None),
        P("tm", None, None),
        P("space", None),
    )
    out_specs = (P("tm", None, "space", None), P("tm", None, "space", None))
    return jax.shard_map(local, mesh=mesh, in_specs=in_specs, out_specs=out_specs, check_vma=False)
```

profile of v0, /device:TPU:6, one launch (start us, length us, event | category | flops | bytes accessed | tf_op | source)
XLA Modules:
  0.0 51.9 jit_solution(15053806812472228050)
XLA Ops:
  0.6 48.2 %shard_map.68 = (f32[3,64,1024]{2,1,0:T(8,128)}, f32[3,64,1024]{2,1,0:T(8,128)}) custom-call(f32[3,64,1024]{2,1,0:T(8,128)} %bitcast.5, f32[3,64,1024]{2,1,0:T(8,128)} %background.1, s32[4,1024]{1,0:T(4,128)} %bitcast.8, f32[4,1024]{1,0:T(4,128)} %bitcast.9, s32[64,1024]{1,0:T(8,128)} %land.1), custom_call_target="tpu_custom_call" | custom-call | tf_op jit(solution)/shard_map/pallas_call | solution.py:414
  48.8 0.0 copy-start
  48.8 2.2 %copy.9 = f32[1,3,64,1024]{3,2,1,0:T(8,128)} copy(f32[1,3,64,1024]{3,2,1,0:T(8,128)} %bitcast.7) | data formatting | bytes 1572864
  51.0 0.0 copy-done
  51.0 0.9 %copy.10 = f32[1,3,64,1024]{3,2,1,0:T(8,128)} copy(f32[1,3,64,1024]{3,2,1,0:T(8,128)S(1)} %bitcast.6) | data formatting | bytes 1572864
Async XLA Ops:
  48.8 2.2 %copy-start = (f32[3,64,1024]{2,1,0:T(8,128)S(1)}, f32[3,64,1024]{2,1,0:T(8,128)}, u32[]{:S(2)}) copy-start(f32[3,64,1024]{2,1,0:T(8,128)} %get-tuple-element.5) | copy-start | bytes 2359300
where the time goes:
time: 52.2 us; the launch traced here: 51.9 us
  Pallas kernels  48.2 us (92%)
  local copies, waits for them, and re-layouts  3.04 us (6%)
  between operations  0.65 us (1%)
    pallas_call x1, Pallas kernels, local(): pl.pallas_call(functools.partial(kernel, n_tm, n_sp), out_shape=(block, b...  48.2 us
    unnamed x4, local copies, waits for them, and re-layouts  3.04 us

commit v1 on v0

v1 whole, which is shorter than its diff:
```python
import functools

import jax
import jax.numpy as jnp
from jax import lax
from jax.experimental import pallas as pl
from jax.experimental.pallas import tpu as pltpu
from jax.sharding import PartitionSpec as P

NSTEP = 4
PAD = 8
LANES = 128

advect = 0.25
gravity = 1.0
coriolis = 0.1
diffuse = 0.1
defect_weight = 2.0
obs_weight = 4.0
step_length = 0.1

KEEP = 1.0 - 4.0 * diffuse
HALF = advect / 2.0
SLOPE = HALF * (advect * gravity / 2.0)

MESH = pl.DeviceIdType.MESH


def kernel(
    n_tm,
    n_sp,
    states,
    background,
    cells_h,
    values_h,
    land,
    gradient,
    nexts,
    xr,
    yr,
    zr,
    prev_end,
    xt,
    yt,
    lam_a,
    lam_b,
    land_i,
    mask,
    dense_x,
    dense_y,
    back,
    cells,
    values,
    cells_n,
    values_n,
    load,
    send,
    recv,
):
    rows, cols = states.shape[1], states.shape[2]
    blocks = cols // LANES
    tm, sp = lax.axis_index("tm"), lax.axis_index("space")
    low, high = 2 * PAD, 2 * PAD + rows
    half_pad = PAD // 2
    has_next, has_next2 = tm < n_tm - 1, tm < n_tm - 2
    has_prev, has_prev2 = tm > 0, tm > 1
    has_up, has_down = sp > 0, sp < n_sp - 1
    every = range(blocks)

    loads = []

    def fetch(src, dst):
        entry = pltpu.make_async_copy(src, dst, load.at[len(loads)])
        entry.start()
        loads.append(entry)

    for c in every:
        part = pl.ds(c * LANES, LANES)
        fetch(states.at[:, :, part], xr.at[:, c, low:high, :])
    n_state = len(loads)
    for c in every:
        part = pl.ds(c * LANES, LANES)
        fetch(land.at[:, part], land_i.at[c, low:high, :])
    fetch(cells_h, cells)
    fetch(values_h, values)
    n_early = len(loads)
    fetch(background, back)

    for start in (0, PAD, high, high + PAD):
        blank = jnp.zeros((3, blocks, PAD, LANES), jnp.float32)
        for ref in (xr, yr, zr):
            ref[:, :, start : start + PAD, :] = blank
        land_i[:, start : start + PAD, :] = jnp.zeros((blocks, PAD, LANES), jnp.int32)

    barrier = pltpu.get_barrier_semaphore()
    near = (
        (has_up, (tm, sp - 1)),
        (has_down, (tm, sp + 1)),
        (has_prev, (tm - 1, sp)),
        (has_next, (tm + 1, sp)),
        (has_prev2, (tm - 2, sp)),
        (has_next2, (tm + 2, sp)),
    )
    for there, device in near:

        @pl.when(there)
        def _(device=device):
            pl.semaphore_signal(barrier, inc=1, device_id=device, device_id_type=MESH)

    for entry in loads[:n_early]:
        entry.wait()
    pl.semaphore_wait(barrier, sum(there.astype(jnp.int32) for there, _ in near))

    started = []

    def start(src, dst, device, sends, receives):
        index = len(started)
        entry = pltpu.make_async_remote_copy(
            src_ref=src,
            dst_ref=dst,
            send_sem=send.at[index],
            recv_sem=recv.at[index],
            device_id=device,
            device_id_type=MESH,
        )

        @pl.when(sends)
        def _():
            entry.start()

        started.append((entry, sends))
        return entry, receives

    def arrive(*pairs):
        for entry, receives in pairs:

            @pl.when(receives)
            def _(entry=entry):
                entry.wait_recv()

    def strip(ref, at):
        return ref.at[:, :, pl.ds(at, PAD), :]

    above, below = (tm, sp - 1), (tm, sp + 1)
    back1, back2, ahead = (tm - 1, sp), (tm - 2, sp), (tm + 1, sp)
    top, bottom, head, tail = PAD, high, low, high - PAD

    halo = [
        start(strip(xr, head), strip(xr, bottom), above, has_up, has_down),
        start(strip(xr, tail), strip(xr, top), below, has_down, has_up),
        start(
            land_i.at[:, pl.ds(head, PAD), :],
            land_i.at[:, pl.ds(bottom, PAD), :],
            above,
            has_up,
            has_down,
        ),
        start(
            land_i.at[:, pl.ds(tail, PAD), :],
            land_i.at[:, pl.ds(top, PAD), :],
            below,
            has_down,
            has_up,
        ),
    ]
    even = lax.rem(tm, 2) == 0
    odd = jnp.logical_not(even)
    obs_next = [
        start(cells, cells_n, back1, has_prev, has_next),
        start(values, values_n, back1, has_prev, has_next),
    ]
    pieces = [low, high - PAD, *range(low + PAD, high - PAD, PAD)]
    n_piece = len(pieces)
    far = [start(strip(xr, p), strip(zr, p), back2, has_prev2, has_next2) for p in pieces]
    direct = [start(strip(xr, p), strip(yr, p), back1, odd, even & has_next) for p in pieces]
    relayed = []

    def relay(count):
        for i in range(len(relayed), min(len(relayed) + count, n_piece)):
            arrive(far[i])
            p = pieces[i]
            relayed.append(
                start(strip(zr, p), strip(yr, p), ahead, even & has_next2, odd & has_next)
            )

    first_row = sp * rows - half_pad
    shift = cols.bit_length() - 1
    tall = rows + PAD
    wide = min(2 * LANES, cols)
    wide_shift = wide.bit_length() - 1
    level = lax.broadcasted_iota(jnp.int32, (tall, cells_h.shape[1]), 0)
    column = lax.broadcasted_iota(jnp.int32, (wide, cells_h.shape[1]), 0)

    def densify(cells, values, dense):
        def one(s, carry):
            cell = cells[pl.ds(s, 1), :]
            value = values[pl.ds(s, 1), :]
            row = lax.shift_right_logical(cell, shift) - first_row
            col = lax.bitwise_and(cell, cols - 1)
            inside = (row >= 0) & (row < tall)
            group = lax.shift_right_logical(col, wide_shift)
            key = jnp.where(inside, group * tall + row, -1)
            lane = lax.bitwise_and(col, wide - 1)
            spread = jnp.where(column == lane, 1.0, 0.0).astype(jnp.bfloat16)
            upper = value.astype(jnp.bfloat16).astype(jnp.float32)
            lower = value - upper
            for g in range(cols // wide):
                hit = level == key - g * tall
                picks = jnp.concatenate(
                    [
                        jnp.where(hit, 1.0, 0.0),
                        jnp.where(hit, upper, 0.0),
                        jnp.where(hit, lower, 0.0),
                    ],
                    axis=0,
                ).astype(jnp.bfloat16)
                out = lax.dot_general(
                    picks, spread, (((1,), (1,)), ((), ())), preferred_element_type=jnp.float32
                )
                count = obs_weight * out[:tall]
                total = count + obs_weight * (out[tall : 2 * tall] + out[2 * tall :])
                for c in range(wide // LANES):
                    at = g * (wide // LANES) + c
                    dense[s, 0, at] = count[:, c * LANES : (c + 1) * LANES]
                    dense[s, 1, at] = total[:, c * LANES : (c + 1) * LANES]
            return carry

        lax.fori_loop(0, NSTEP, one, 0)

    lane_at = lax.broadcasted_iota(jnp.int32, (PAD, LANES), 1)
    is_first, is_last = lane_at == 0, lane_at == LANES - 1

    def from_right(tiles):
        turned = [pltpu.roll(tile, LANES - 1, 1) for tile in tiles]
        return [jnp.where(is_last, turned[(c + 1) % blocks], turned[c]) for c in every]

    def from_left(tiles):
        turned = [pltpu.roll(tile, 1, 1) for tile in tiles]
        return [jnp.where(is_first, turned[c - 1], turned[c]) for c in every]

    def tile_loop(begin, count, unroll, body):
        def group(i, carry):
            for j in range(unroll):
                body(begin + (i * unroll + j) * PAD)
            return carry

        lax.fori_loop(0, count // unroll, group, 0)

    def parts(count):
        return max(u for u in (4, 3, 2, 1) if count % u == 0 and u <= 3)

    def edges(ref, fill):
        for there, at in ((has_up, top), (has_down, bottom)):

            @pl.when(jnp.logical_not(there))
            def _(at=at):
                for field in range(3):
                    value = jnp.full((blocks, PAD, LANES), fill[field], jnp.float32)
                    ref[field, :, at : at + PAD, :] = value

    def transform(raw, ref, first, last):
        def one(r):
            r = pl.multiple_of(r, PAD)
            here = pl.ds(r, PAD)
            for c in every:
                ref[0, c, here, :] = 1.0 + raw[0, c, here, :]
                ref[1, c, here, :] = HALF * raw[1, c, here, :]
                ref[2, c, here, :] = HALF * raw[2, c, here, :]

        count = (last - first) // PAD
        tile_loop(first, count, parts(count), one)

    def forward_tile(src, dst, r):
        here, up, down = pl.ds(r, PAD), pl.ds(r - 1, PAD), pl.ds(r + 1, PAD)
        q = [src[0, c, here, :] for c in every]
        u = [src[1, c, here, :] for c in every]
        v = [src[2, c, here, :] for c in every]
        slope = [SLOPE * q[c] for c in every]
        mixed = [diffuse * u[c] for c in every]
        q_right = from_right([q[c] * (diffuse - u[c]) for c in every])
        q_left = from_left([q[c] * (diffuse + u[c]) for c in every])
        u_right = from_right([mixed[c] - slope[c] for c in every])
        u_left = from_left([mixed[c] + slope[c] for c in every])
        v_right = from_right(v)
        v_left = from_left(v)
        for c in every:
            m = mask[c, here, :]
            q_up, q_down = src[0, c, up, :], src[0, c, down, :]
            v_up, v_down = src[2, c, up, :], src[2, c, down, :]
            u_sum = src[1, c, up, :] + src[1, c, down, :]
            dst[0, c, here, :] = (
                KEEP * q[c]
                + (q_right[c] + q_left[c])
                + (q_up * (diffuse + v_up) + q_down * (diffuse - v_down))
            )
            dst[1, c, here, :] = m * (
                KEEP * u[c] + coriolis * v[c] + (u_right[c] + u_left[c]) + diffuse * u_sum
            )
            dst[2, c, here, :] = m * (
                KEEP * v[c]
                - coriolis * u[c]
                + diffuse * ((v_right[c] + v_left[c]) + (v_up + v_down))
                + SLOPE * (q_up - q_down)
            )

    def forward(levels):
        full = (rows + 2 * PAD) // PAD

        def step(s, carry):
            src, dst = levels.at[s], levels.at[s + 1]
            tile_loop(top, full, parts(full), lambda r: forward_tile(src, dst, r))
            edges(dst, (1.0, 0.0, 0.0))
            return carry

        lax.fori_loop(0, NSTEP - 1, step, 0)
        src, dst = levels.at[NSTEP - 1], levels.at[NSTEP]
        count = full - 1
        tile_loop(top + half_pad, count, parts(count), lambda r: forward_tile(src, dst, r))
        edges(dst, (1.0, 0.0, 0.0))

    n_seed = (rows + PAD) // PAD
    seed_at = top + half_pad

    def drop(r):
        return pl.ds(pl.multiple_of(r - seed_at, PAD), PAD)

    def begin(levels, following, there, dense, lam):
        ends = levels.at[NSTEP]
        weight = jnp.where(there, defect_weight, 0.0)

        def one(r):
            here, at = pl.ds(r, PAD), drop(r)
            for c in every:
                m = mask[c, here, :]
                raw = [jnp.where(there, following[f, c, here, :], 0.0) for f in range(3)]
                pull = weight + dense[NSTEP - 1, 0, c, at, :]
                lam[0, c, here, :] = (
                    pull * ends[0, c, here, :]
                    - (weight + dense[NSTEP - 1, 1, c, at, :])
                    - weight * raw[0]
                )
                for f in (1, 2):
                    gap = (weight / (HALF * HALF)) * ends[f, c, here, :]
                    lam[f, c, here, :] = m * (gap - (weight / HALF) * raw[f])

        tile_loop(seed_at, n_seed, parts(n_seed), one)
        edges(lam, (0.0, 0.0, 0.0))

    def adjoint_tile(src, state, r):
        here, up, down = pl.ds(r, PAD), pl.ds(r - 1, PAD), pl.ds(r + 1, PAD)
        a = [src[0, c, here, :] for c in every]
        b = [src[1, c, here, :] for c in every]
        e = [src[2, c, here, :] for c in every]
        a_right, a_left = from_right(a), from_left(a)
        b_right, b_left = from_right(b), from_left(b)
        e_right, e_left = from_right(e), from_left(e)
        out = []
        for c in every:
            a_up, a_down = src[0, c, up, :], src[0, c, down, :]
            e_up, e_down = src[2, c, up, :], src[2, c, down, :]
            b_sum = src[1, c, up, :] + src[1, c, down, :]
            across, along = a_right[c] - a_left[c], a_down - a_up
            q = state[0, c, here, :]
            lam_q = (
                KEEP * a[c]
                + diffuse * ((a_right[c] + a_left[c]) + (a_up + a_down))
                + (state[1, c, here, :] * across + state[2, c, here, :] * along)
                + SLOPE * ((b_right[c] - b_left[c]) + (e_down - e_up))
            )
            lam_u = (
                KEEP * b[c]
                + diffuse * ((b_right[c] + b_left[c]) + b_sum)
                + q * across
                - coriolis * e[c]
            )
            lam_v = (
                KEEP * e[c]
                + diffuse * ((e_right[c] + e_left[c]) + (e_up + e_down))
                + q * along
                + coriolis * b[c]
            )
            out.append((lam_q, lam_u, lam_v))
        return out

    def adjoint(levels, dense):
        src, dst = lam_a, lam_b
        for s in reversed(range(1, NSTEP)):

            def one(r, src=src, dst=dst, s=s):
                here, at = pl.ds(r, PAD), drop(r)
                out = adjoint_tile(src, levels.at[s], r)
                for c in every:
                    m = mask[c, here, :]
                    push = dense[s - 1, 0, c, at, :] * levels[s, 0, c, here, :]
                    dst[0, c, here, :] = out[c][0] + (push - dense[s - 1, 1, c, at, :])
                    dst[1, c, here, :] = m * out[c][1]
                    dst[2, c, here, :] = m * out[c][2]

            tile_loop(seed_at, n_seed, parts(n_seed), one)
            edges(dst, (0.0, 0.0, 0.0))
            src, dst = dst, src
        return src

    n_row = rows // PAD
    row_unroll = 2 if n_row % 2 == 0 else 1

    def inside(r):
        return pl.ds(pl.multiple_of(r - low, PAD), PAD)

    def block(c):
        return pl.ds(c * LANES, LANES)

    densify(cells, values, dense_x)
    arrive(*halo)

    def to_mask(r):
        here = pl.ds(pl.multiple_of(r, PAD), PAD)
        for c in every:
            mask[c, here, :] = land_i[c, here, :].astype(jnp.float32)

    full = (rows + 2 * PAD) // PAD
    tile_loop(top, full, parts(full), to_mask)
    transform(xr, xt.at[0], top, high + PAD)
    for levels in (xt, yt):
        for at in (0, high + PAD):
            levels[0, :, :, at : at + PAD, :] = jnp.zeros((3, blocks, PAD, LANES), jnp.float32)
    relay(2)
    forward(xt)
    relay(2)
    arrive(*obs_next)
    densify(cells_n, values_n, dense_y)
    relay(2)
    arrive(*direct[:2], *relayed[:2])
    next_up = has_next & has_up
    next_down = has_next & has_down
    next2_up = has_next2 & has_up
    next2_down = has_next2 & has_down
    halo_next = [
        start(strip(yr, head), strip(yr, bottom), above, next_up, next_down),
        start(strip(yr, tail), strip(yr, top), below, next_down, next_up),
    ]
    halo_far = [
        start(strip(zr, head), strip(zr, bottom), above, next2_up, next2_down),
        start(strip(zr, tail), strip(zr, top), below, next2_down, next2_up),
    ]
    relay(n_piece)
    ends = start(
        xt.at[NSTEP, :, :, pl.ds(low, rows), :], prev_end, ahead, has_next, has_prev
    )
    arrive(*direct[2:], *relayed[2:], *halo_next)

    begin(xt, yr, has_next, dense_x, lam_a)
    last = adjoint(xt, dense_x)

    def own(r):
        out = adjoint_tile(last, xt.at[0], r)
        at = inside(r)
        for c in every:
            gradient[0, at, block(c)] = out[c][0]
            gradient[1, at, block(c)] = HALF * out[c][1]
            gradient[2, at, block(c)] = HALF * out[c][2]

    tile_loop(low, n_row, row_unroll, own)

    transform(yr, yt.at[0], top, high + PAD)
    forward(yt)
    arrive(*halo_far)
    begin(yt, zr, has_next2, dense_y, lam_a)
    last = adjoint(yt, dense_y)

    def raw_end(ref, f, c, here):
        value = ref[f, c, here, :]
        return value - 1.0 if f == 0 else (1.0 / HALF) * value

    def other(r):
        out = adjoint_tile(last, yt.at[0], r)
        here = pl.ds(pl.multiple_of(r, PAD), PAD)
        at = inside(r)
        for c in every:
            for f in range(3):
                state = yr[f, c, here, :]
                end = raw_end(xt.at[NSTEP], f, c, here)
                lam = out[c][f] if f == 0 else HALF * out[c][f]
                grad = defect_weight * (state - end) + lam
                nexts[f, at, block(c)] = jnp.where(has_next, state - step_length * grad, end)

    tile_loop(low, n_row, row_unroll, other)

    arrive(ends)
    for entry in loads[n_early:]:
        entry.wait()

    def finish(r):
        here = pl.ds(pl.multiple_of(r, PAD), PAD)
        at = inside(r)
        for c in every:
            for f in range(3):
                before = jnp.where(
                    has_prev, raw_end(prev_end, f, c, at), back[f, at, block(c)]
                )
                defect = xr[f, c, here, :] - before
                gradient[f, at, block(c)] = gradient[f, at, block(c)] + defect_weight * defect

    tile_loop(low, n_row, 1, finish)

    for entry, sends in started:

        @pl.when(sends)
        def _(entry=entry):
            entry.wait_send()


def solution(mesh):
    n_tm, n_sp = mesh.shape["tm"], mesh.shape["space"]

    def local(states, background, obs_cells, obs_values, land_mask):
        _, fields, rows, cols = states.shape
        padded = rows + 4 * PAD
        blocks = cols // LANES
        block = pltpu.VMEM((fields, rows, cols), jnp.float32)
        f32 = functools.partial(pltpu.VMEM, dtype=jnp.float32)
        i32 = functools.partial(pltpu.VMEM, dtype=jnp.int32)
        n_copy = 11 + 3 * (rows // PAD)
        gradient, nexts = pl.pallas_call(
            functools.partial(kernel, n_tm, n_sp),
            out_shape=(block, block),
            in_specs=[pl.BlockSpec(memory_space=pl.ANY)] * 5,
            out_specs=(pl.BlockSpec(memory_space=pltpu.VMEM),) * 2,
            scratch_shapes=[
                f32((fields, blocks, padded, LANES)),
                f32((fields, blocks, padded, LANES)),
                f32((fields, blocks, padded, LANES)),
                f32((fields, blocks, rows, LANES)),
                f32((NSTEP + 1, fields, blocks, padded, LANES)),
                f32((NSTEP + 1, fields, blocks, padded, LANES)),
                f32((fields, blocks, padded, LANES)),
                f32((fields, blocks, padded, LANES)),
                i32((blocks, padded, LANES)),
                f32((blocks, padded, LANES)),
                f32((NSTEP, 2, blocks, rows + PAD, LANES)),
                f32((NSTEP, 2, blocks, rows + PAD, LANES)),
                f32((fields, rows, cols)),
                i32(obs_cells.shape[1:]),
                f32(obs_values.shape[1:]),
                i32(obs_cells.shape[1:]),
                f32(obs_values.shape[1:]),
                pltpu.SemaphoreType.DMA((2 * blocks + 3,)),
                pltpu.SemaphoreType.DMA((n_copy,)),
                pltpu.SemaphoreType.DMA((n_copy,)),
            ],
            compiler_params=pltpu.CompilerParams(
                collective_id=0, has_side_effects=True, vmem_limit_bytes=44 * 2**20
            ),
        )(states[0], background, obs_cells[0], obs_values[0], land_mask)
        return gradient[None], nexts[None]

    in_specs = (
        P("tm", None, "space", None),
        P(None, "space", None),
        P("tm", None, None),
        P("tm", None, None),
        P("space", None),
    )
    out_specs = (P("tm", None, "space", None), P("tm", None, "space", None))
    return jax.shard_map(local, mesh=mesh, in_specs=in_specs, out_specs=out_specs, check_vma=False)
```

time: 52.2 us -> 51.9 us (level)
  Pallas kernels: 48.2 us -> 44.1 us
  local copies, waits for them, and re-layouts: 3.04 us -> 6.4 us
    pallas_call x1, Pallas kernels: 48.2 us -> 44.1 us  [local(): pl.pallas_call(functools.partial(kernel, n_tm, n_sp), out_shape=(block, b...]
    unnamed x4 -> x12, local copies, waits for them, and re-layouts: 3.04 us -> 6.4 us
where the time goes in v1:
time: 51.9 us; the launch traced here: 51.2 us
  Pallas kernels  44.1 us (85%)
  local copies, waits for them, and re-layouts  6.4 us (12%)
  between operations  0.65 us (1%)
    pallas_call x1, Pallas kernels, local(): pl.pallas_call(functools.partial(kernel, n_tm, n_sp), out_shape=(block, b...  44.1 us
    unnamed x12, local copies, waits for them, and re-layouts  6.4 us

profile of v1, /device:TPU:6, one launch (start us, length us, event | category | flops | bytes accessed | tf_op | source)
XLA Modules:
  0.0 51.2 jit_solution(3374540267335175629)
XLA Ops:
  0.6 0.0 copy-start
  0.6 1.1 %copy-done = f32[1,3,64,1024]{3,2,1,0:T(8,128)S(1)} copy-done((f32[1,3,64,1024]{3,2,1,0:T(8,128)S(1)}, f32[1,3,64,1024]{3,2,1,0:T(8,128)}, u32[]{:S(2)}) %copy-start) | copy-done | bytes 786456
  1.8 0.0 copy-start.1
  1.8 1.1 %copy-done.1 = f32[3,64,1024]{2,1,0:T(8,128)S(1)} copy-done((f32[3,64,1024]{2,1,0:T(8,128)S(1)}, f32[3,64,1024]{2,1,0:T(8,128)}, u32[]{:S(2)}) %copy-start.1) | copy-done | bytes 786456
  2.9 0.0 copy-start.2
  2.9 0.9 %copy-done.2 = s32[64,1024]{1,0:T(8,128)S(1)} copy-done((s32[64,1024]{1,0:T(8,128)S(1)}, s32[64,1024]{1,0:T(8,128)}, u32[]{:S(2)}) %copy-start.2) | copy-done | bytes 262168
  3.8 0.0 copy-start.3
  3.9 0.7 %copy-done.3 = s32[1,4,1024]{2,1,0:T(4,128)S(1)} copy-done((s32[1,4,1024]{2,1,0:T(4,128)S(1)}, s32[1,4,1024]{2,1,0:T(4,128)}, u32[]{:S(2)}) %copy-start.3) | copy-done | bytes 16408
  4.6 0.0 copy-start.4
  4.6 0.7 %copy-done.4 = f32[1,4,1024]{2,1,0:T(4,128)S(1)} copy-done((f32[1,4,1024]{2,1,0:T(4,128)S(1)}, f32[1,4,1024]{2,1,0:T(4,128)}, u32[]{:S(2)}) %copy-start.4) | copy-done | bytes 16408
  5.3 44.1 %shard_map.68 = (f32[3,64,1024]{2,1,0:T(8,128)S(1)}, f32[3,64,1024]{2,1,0:T(8,128)S(1)}) custom-call(f32[3,64,1024]{2,1,0:T(8,128)S(1)} %bitcast.7, f32[3,64,1024]{2,1,0:T(8,128)S(1)} %copy-done.1, s32[4,1024]{1,0:T(4,128)S(1)} %bitcast.8, f32[4,1024]{1,0:T(4,128)S(1)} %bitcast.9, s32[64,1024]{1,0:T(8,128)S(1)} %copy-done.2), custom_call_target="tpu_custom_call" | custom-call | tf_op jit(solution)/shard_map/pallas_call | solution.py:524
  49.4 0.9 %copy.9 = f32[1,3,64,1024]{3,2,1,0:T(8,128)} copy(f32[1,3,64,1024]{3,2,1,0:T(8,128)S(1)} %bitcast.6) | data formatting | bytes 1572864
  50.3 0.9 %copy.10 = f32[1,3,64,1024]{3,2,1,0:T(8,128)} copy(f32[1,3,64,1024]{3,2,1,0:T(8,128)S(1)} %bitcast.5) | data formatting | bytes 1572864
Async XLA Ops:
  0.6 1.1 %copy-start = (f32[1,3,64,1024]{3,2,1,0:T(8,128)S(1)}, f32[1,3,64,1024]{3,2,1,0:T(8,128)}, u32[]{:S(2)}) copy-start(f32[1,3,64,1024]{3,2,1,0:T(8,128)} %param.5) | copy-start | bytes 2359300
  1.8 1.1 %copy-start.1 = (f32[3,64,1024]{2,1,0:T(8,128)S(1)}, f32[3,64,1024]{2,1,0:T(8,128)}, u32[]{:S(2)}) copy-start(f32[3,64,1024]{2,1,0:T(8,128)} %background.1) | copy-start | bytes 2359300
  2.9 0.9 %copy-start.2 = (s32[64,1024]{1,0:T(8,128)S(1)}, s32[64,1024]{1,0:T(8,128)}, u32[]{:S(2)}) copy-start(s32[64,1024]{1,0:T(8,128)} %land.1) | copy-start | bytes 786436
  3.8 0.7 %copy-start.3 = (s32[1,4,1024]{2,1,0:T(4,128)S(1)}, s32[1,4,1024]{2,1,0:T(4,128)}, u32[]{:S(2)}) copy-start(s32[1,4,1024]{2,1,0:T(4,128)} %param.7) | copy-start | bytes 49156
  4.6 0.7 %copy-start.4 = (f32[1,4,1024]{2,1,0:T(4,128)S(1)}, f32[1,4,1024]{2,1,0:T(4,128)}, u32[]{:S(2)}) copy-start(f32[1,4,1024]{2,1,0:T(4,128)} %param.8) | copy-start | bytes 49156

commit v2 on v1

--- a/solution.py
+++ b/solution.py
@@ -10,6 +10,7 @@
 NSTEP = 4
 PAD = 8
 LANES = 128
+DETOUR = 3
 
 advect = 0.25
 gravity = 1.0
@@ -39,9 +40,11 @@
     xr,
     yr,
     zr,
+    cr,
     prev_end,
     xt,
     yt,
+    ct,
     lam_a,
     lam_b,
     land_i,
@@ -88,7 +91,7 @@
 
     for start in (0, PAD, high, high + PAD):
         blank = jnp.zeros((3, blocks, PAD, LANES), jnp.float32)
-        for ref in (xr, yr, zr):
+        for ref in (xr, yr, zr, cr):
             ref[:, :, start : start + PAD, :] = blank
         land_i[:, start : start + PAD, :] = jnp.zeros((blocks, PAD, LANES), jnp.int32)
 
@@ -101,6 +104,8 @@
         (has_prev2, (tm - 2, sp)),
         (has_next2, (tm + 2, sp)),
     )
+    if n_tm > DETOUR:
+        near += ((tm == 0, (tm + DETOUR, sp)), (tm == DETOUR, (tm - DETOUR, sp)))
     for there, device in near:
 
         @pl.when(there)
@@ -142,7 +147,8 @@
         return ref.at[:, :, pl.ds(at, PAD), :]
 
     above, below = (tm, sp - 1), (tm, sp + 1)
-    back1, back2, ahead = (tm - 1, sp), (tm - 2, sp), (tm + 1, sp)
+    back1, back2 = (tm - 1, sp), (tm - 2, sp)
+    ahead, ahead2 = (tm + 1, sp), (tm + 2, sp)
     top, bottom, head, tail = PAD, high, low, high - PAD
 
     halo = [
@@ -173,15 +179,17 @@
     n_piece = len(pieces)
     far = [start(strip(xr, p), strip(zr, p), back2, has_prev2, has_next2) for p in pieces]
     direct = [start(strip(xr, p), strip(yr, p), back1, odd, even & has_next) for p in pieces]
-    relayed = []
-
-    def relay(count):
+    relayed, carried = [], []
+
+    def serve(count):
         for i in range(len(relayed), min(len(relayed) + count, n_piece)):
+            p = pieces[i]
             arrive(far[i])
-            p = pieces[i]
             relayed.append(
                 start(strip(zr, p), strip(yr, p), ahead, even & has_next2, odd & has_next)
             )
+            arrive(direct[i], relayed[i])
+            carried.append(start(strip(yr, p), strip(cr, p), ahead2, has_next2, has_prev2))
 
     first_row = sp * rows - half_pad
     shift = cols.bit_length() - 1
@@ -191,7 +199,7 @@
     level = lax.broadcasted_iota(jnp.int32, (tall, cells_h.shape[1]), 0)
     column = lax.broadcasted_iota(jnp.int32, (wide, cells_h.shape[1]), 0)
 
-    def densify(cells, values, dense):
+    def densify(cells, values, dense, begin_at, end_at):
         def one(s, carry):
             cell = cells[pl.ds(s, 1), :]
             value = values[pl.ds(s, 1), :]
@@ -225,7 +233,7 @@
                     dense[s, 1, at] = total[:, c * LANES : (c + 1) * LANES]
             return carry
 
-        lax.fori_loop(0, NSTEP, one, 0)
+        lax.fori_loop(begin_at, end_at, one, 0)
 
     lane_at = lax.broadcasted_iota(jnp.int32, (PAD, LANES), 1)
     is_first, is_last = lane_at == 0, lane_at == LANES - 1
@@ -410,7 +418,7 @@
     def block(c):
         return pl.ds(c * LANES, LANES)
 
-    densify(cells, values, dense_x)
+    densify(cells, values, dense_x, 0, NSTEP)
     arrive(*halo)
 
     def to_mask(r):
@@ -421,20 +429,18 @@
     full = (rows + 2 * PAD) // PAD
     tile_loop(top, full, parts(full), to_mask)
     transform(xr, xt.at[0], top, high + PAD)
-    for levels in (xt, yt):
+    for levels in (xt, yt, ct):
         for at in (0, high + PAD):
             levels[0, :, :, at : at + PAD, :] = jnp.zeros((3, blocks, PAD, LANES), jnp.float32)
-    relay(2)
+    serve(1)
     forward(xt)
-    relay(2)
-    arrive(*obs_next)
-    densify(cells_n, values_n, dense_y)
-    relay(2)
-    arrive(*direct[:2], *relayed[:2])
+    serve(1)
     next_up = has_next & has_up
     next_down = has_next & has_down
     next2_up = has_next2 & has_up
     next2_down = has_next2 & has_down
+    prev2_up = has_prev2 & has_up
+    prev2_down = has_prev2 & has_down
     halo_next = [
         start(strip(yr, head), strip(yr, bottom), above, next_up, next_down),
         start(strip(yr, tail), strip(yr, top), below, next_down, next_up),
@@ -443,11 +449,40 @@
         start(strip(zr, head), strip(zr, bottom), above, next2_up, next2_down),
         start(strip(zr, tail), strip(zr, top), below, next2_down, next2_up),
     ]
-    relay(n_piece)
-    ends = start(
-        xt.at[NSTEP, :, :, pl.ds(low, rows), :], prev_end, ahead, has_next, has_prev
-    )
-    arrive(*direct[2:], *relayed[2:], *halo_next)
+    arrive(*obs_next)
+    serve(1)
+    densify(cells_n, values_n, dense_y, 0, NSTEP // 2)
+    serve(1)
+    densify(cells_n, values_n, dense_y, NSTEP // 2, NSTEP)
+    serve(1)
+    arrive(*carried[:2])
+    halo_carried = [
+        start(strip(cr, head), strip(cr, bottom), above, prev2_up, prev2_down),
+        start(strip(cr, tail), strip(cr, top), below, prev2_down, prev2_up),
+    ]
+    serve(n_piece)
+    n_far = n_piece * 3 // 8 if n_tm > DETOUR else 0
+    via = [
+        start(
+            strip(xt.at[NSTEP], p),
+            strip(prev_end, p - low),
+            (tm + DETOUR, sp),
+            tm == 0,
+            tm == DETOUR,
+        )
+        for p in pieces[n_piece - n_far :]
+    ]
+    ends = [
+        start(strip(xt.at[NSTEP], p), strip(prev_end, p - low), ahead, tm == 0, tm == 1)
+        for p in pieces[: n_piece - n_far]
+    ]
+    arrive(*halo_next)
+
+    def detour():
+        for i, p in enumerate(pieces[n_piece - n_far :]):
+            arrive(via[i])
+            at = strip(prev_end, p - low)
+            ends.append(start(at, at, back2, tm == DETOUR, tm == 1))
 
     begin(xt, yr, has_next, dense_x, lam_a)
     last = adjoint(xt, dense_x)
@@ -486,22 +521,50 @@
 
     tile_loop(low, n_row, row_unroll, other)
 
-    arrive(ends)
+    arrive(*carried[2:], *halo_carried)
+
+    @pl.when(has_prev2)
+    def _():
+        transform(cr, ct.at[0], top, high + PAD)
+        src, dst = ct.at[0], ct.at[1]
+        for s in range(NSTEP - 1):
+            tile_loop(
+                seed_at,
+                n_seed,
+                parts(n_seed),
+                lambda r, src=src, dst=dst: forward_tile(src, dst, r),
+            )
+            edges(dst, (1.0, 0.0, 0.0))
+            src, dst = dst, src
+        tile_loop(low, n_row, row_unroll, lambda r: forward_tile(src, dst, r))
+
+    detour()
+    arrive(*ends)
     for entry in loads[n_early:]:
         entry.wait()
 
-    def finish(r):
-        here = pl.ds(pl.multiple_of(r, PAD), PAD)
-        at = inside(r)
-        for c in every:
-            for f in range(3):
-                before = jnp.where(
-                    has_prev, raw_end(prev_end, f, c, at), back[f, at, block(c)]
-                )
-                defect = xr[f, c, here, :] - before
-                gradient[f, at, block(c)] = gradient[f, at, block(c)] + defect_weight * defect
-
-    tile_loop(low, n_row, 1, finish)
+    def finish(before):
+        def one(r):
+            here = pl.ds(pl.multiple_of(r, PAD), PAD)
+            at = inside(r)
+            for c in every:
+                for f in range(3):
+                    defect = xr[f, c, here, :] - before(f, c, here, at)
+                    gradient[f, at, block(c)] = gradient[f, at, block(c)] + defect_weight * defect
+
+        tile_loop(low, n_row, 1, one)
+
+    @pl.when(has_prev2)
+    def _():
+        finish(lambda f, c, here, at: raw_end(ct.at[NSTEP % 2], f, c, here))
+
+    @pl.when(tm == 1)
+    def _():
+        finish(lambda f, c, here, at: raw_end(prev_end, f, c, at))
+
+    @pl.when(tm == 0)
+    def _():
+        finish(lambda f, c, here, at: back[f, at, block(c)])
 
     for entry, sends in started:
 
@@ -520,7 +583,7 @@
         block = pltpu.VMEM((fields, rows, cols), jnp.float32)
         f32 = functools.partial(pltpu.VMEM, dtype=jnp.float32)
         i32 = functools.partial(pltpu.VMEM, dtype=jnp.int32)
-        n_copy = 11 + 3 * (rows // PAD)
+        n_copy = 12 + 6 * (rows // PAD)
         gradient, nexts = pl.pallas_call(
             functools.partial(kernel, n_tm, n_sp),
             out_shape=(block, block),
@@ -530,9 +593,11 @@
                 f32((fields, blocks, padded, LANES)),
                 f32((fields, blocks, padded, LANES)),
                 f32((fields, blocks, padded, LANES)),
+                f32((fields, blocks, padded, LANES)),
                 f32((fields, blocks, rows, LANES)),
                 f32((NSTEP + 1, fields, blocks, padded, LANES)),
                 f32((NSTEP + 1, fields, blocks, padded, LANES)),
+                f32((2, fields, blocks, padded, LANES)),
                 f32((fields, blocks, padded, LANES)),
                 f32((fields, blocks, padded, LANES)),
                 i32((blocks, padded, LANES)),

time: 51.9 us -> 62.5 us (1.20)
  Pallas kernels: 44.1 us -> 55.1 us
    pallas_call x1, Pallas kernels: 44.1 us -> 55.1 us  [local(): pl.pallas_call(functools.partial(kernel, n_tm, n_sp), out_shape=(block, b...]
where the time goes in v2:
time: 62.5 us; the launch traced here: 62.2 us
  Pallas kernels  55.1 us (88%)
  local copies, waits for them, and re-layouts  6.4 us (10%)
  between operations  0.65 us (1%)
    pallas_call x1, Pallas kernels, local(): pl.pallas_call(functools.partial(kernel, n_tm, n_sp), out_shape=(block, b...  55.1 us
    unnamed x12, local copies, waits for them, and re-layouts  6.4 us

profile of v2, /device:TPU:6, one launch (start us, length us, event | category | flops | bytes accessed | tf_op | source)
XLA Modules:
  0.0 62.2 jit_solution(5317815059519345793)
XLA Ops:
  0.6 0.0 copy-start
  0.6 1.1 %copy-done = f32[1,3,64,1024]{3,2,1,0:T(8,128)S(1)} copy-done((f32[1,3,64,1024]{3,2,1,0:T(8,128)S(1)}, f32[1,3,64,1024]{3,2,1,0:T(8,128)}, u32[]{:S(2)}) %copy-start) | copy-done | bytes 786456
  1.8 0.0 copy-start.1
  1.8 1.1 %copy-done.1 = f32[3,64,1024]{2,1,0:T(8,128)S(1)} copy-done((f32[3,64,1024]{2,1,0:T(8,128)S(1)}, f32[3,64,1024]{2,1,0:T(8,128)}, u32[]{:S(2)}) %copy-start.1) | copy-done | bytes 786456
  2.9 0.0 copy-start.2
  2.9 0.9 %copy-done.2 = s32[64,1024]{1,0:T(8,128)S(1)} copy-done((s32[64,1024]{1,0:T(8,128)S(1)}, s32[64,1024]{1,0:T(8,128)}, u32[]{:S(2)}) %copy-start.2) | copy-done | bytes 262168
  3.8 0.0 copy-start.3
  3.9 0.7 %copy-done.3 = s32[1,4,1024]{2,1,0:T(4,128)S(1)} copy-done((s32[1,4,1024]{2,1,0:T(4,128)S(1)}, s32[1,4,1024]{2,1,0:T(4,128)}, u32[]{:S(2)}) %copy-start.3) | copy-done | bytes 16408
  4.6 0.0 copy-start.4
  4.6 0.7 %copy-done.4 = f32[1,4,1024]{2,1,0:T(4,128)S(1)} copy-done((f32[1,4,1024]{2,1,0:T(4,128)S(1)}, f32[1,4,1024]{2,1,0:T(4,128)}, u32[]{:S(2)}) %copy-start.4) | copy-done | bytes 16408
  5.3 55.1 %shard_map.68 = (f32[3,64,1024]{2,1,0:T(8,128)S(1)}, f32[3,64,1024]{2,1,0:T(8,128)S(1)}) custom-call(f32[3,64,1024]{2,1,0:T(8,128)S(1)} %bitcast.7, f32[3,64,1024]{2,1,0:T(8,128)S(1)} %copy-done.1, s32[4,1024]{1,0:T(4,128)S(1)} %bitcast.8, f32[4,1024]{1,0:T(4,128)S(1)} %bitcast.9, s32[64,1024]{1,0:T(8,128)S(1)} %copy-done.2), custom_call_target="tpu_custom_call" | custom-call | tf_op jit(solution)/shard_map/pallas_call | solution.py:587
  60.4 0.9 %copy.9 = f32[1,3,64,1024]{3,2,1,0:T(8,128)} copy(f32[1,3,64,1024]{3,2,1,0:T(8,128)S(1)} %bitcast.6) | data formatting | bytes 1572864
  61.3 0.9 %copy.10 = f32[1,3,64,1024]{3,2,1,0:T(8,128)} copy(f32[1,3,64,1024]{3,2,1,0:T(8,128)S(1)} %bitcast.5) | data formatting | bytes 1572864
Async XLA Ops:
  0.6 1.1 %copy-start = (f32[1,3,64,1024]{3,2,1,0:T(8,128)S(1)}, f32[1,3,64,1024]{3,2,1,0:T(8,128)}, u32[]{:S(2)}) copy-start(f32[1,3,64,1024]{3,2,1,0:T(8,128)} %param.5) | copy-start | bytes 2359300
  1.8 1.1 %copy-start.1 = (f32[3,64,1024]{2,1,0:T(8,128)S(1)}, f32[3,64,1024]{2,1,0:T(8,128)}, u32[]{:S(2)}) copy-start(f32[3,64,1024]{2,1,0:T(8,128)} %background.1) | copy-start | bytes 2359300
  2.9 0.9 %copy-start.2 = (s32[64,1024]{1,0:T(8,128)S(1)}, s32[64,1024]{1,0:T(8,128)}, u32[]{:S(2)}) copy-start(s32[64,1024]{1,0:T(8,128)} %land.1) | copy-start | bytes 786436
  3.8 0.7 %copy-start.3 = (s32[1,4,1024]{2,1,0:T(4,128)S(1)}, s32[1,4,1024]{2,1,0:T(4,128)}, u32[]{:S(2)}) copy-start(s32[1,4,1024]{2,1,0:T(4,128)} %param.7) | copy-start | bytes 49156
  4.6 0.7 %copy-start.4 = (f32[1,4,1024]{2,1,0:T(4,128)S(1)}, f32[1,4,1024]{2,1,0:T(4,128)}, u32[]{:S(2)}) copy-start(f32[1,4,1024]{2,1,0:T(4,128)} %param.8) | copy-start | bytes 49156
